TPU v7x, 32 devices: a whole 2x2x4 slice. The times are simulated.
32 devices in a mesh: scen: 2 (over x), gx: 16 (over z, y, core).
Axes of the slice: x: 2, y: 2, z: 4, core: 2. Of those that a mesh axis runs over, the one named last changes fastest.
Arguments:
- populations: float32 [54, 16, 4, 8, 256], P('scen', 'gx'), parts along dimension 0, may hold values from 0.15 to 2
- cell_kind: int32 [16, 4, 8, 512], P('gx', None, None, 'scen'), parts along dimension 3, may hold values from 0 to 4, as said below
- profile: int32 [16, 4, 8, 512], P('gx', None, None, 'scen'), parts along dimension 3, may hold values from 0 to 7
- vent_table: float32 [16, 3], P('scen'), parts along dimension 0, may hold values from -0.08 to 0.08
- rates: float32 [27], replicated, may hold values from 1 to 1.9
Outputs:
- advanced: float32 [54, 16, 4, 8, 256], P('scen', 'gx'), parts along dimension 0
There are 2 independent parts, one for each index of `scen`. A program takes and returns all parts, laid end to end along the dimension named above; an argument that names none is the same for every part. Nothing has to cross between parts.
Inputs may be any that keep to these rules, and one draw needn't show every extreme that they name: `cell_kind`: 0 fluid, 1 wall, 2 vent, 3 inflow, 4 outflow.
All inputs are finite; a program needn't handle non-finite values.
Results may differ from a plain program's by a relative error of at most 0.0003.
Values sent between devices are 32-bit elements; how exact they have to be, the bound alone decides.
A program may use at most 64 MiB of HBM per device.

v0:
```python
import jax
import jax.numpy as jnp
from jax import lax
from jax.experimental import pallas as pl
from jax.experimental.pallas import tpu as pltpu
from jax.sharding import PartitionSpec as P

PY = 8
STEPS = 3
BIG = 1e30
MESH = pl.DeviceIdType.MESH
VELOCITIES = [(a, b, e) for a in (-1, 0, 1) for b in (-1, 0, 1) for e in (-1, 0, 1)]


def spread(low, mid, high):
    even = low + high
    return even + 4.0 * mid, high - low, even


def gather_back(zeroth, first, second):
    return second - first, zeroth - 0.5 * second, second + first


def along_axes(values, transform):
    values = list(values)
    for stride in (1, 3, 9):
        for start in range(27):
            if (start // stride) % 3 == 0:
                picks = [start, start + stride, start + 2 * stride]
                done = transform(*[values[i] for i in picks])
                for i, value in zip(picks, done):
                    values[i] = value
    return values


def collide(g, rates):
    m = along_axes(g, spread)
    rho, jx, jy, jz = m[0], m[9], m[3], m[1]
    inverse = 1.0 / rho
    u = (jx * inverse, jy * inverse, jz * inverse)
    j = (jx, jy, jz)
    sq = [3.0 * (j[d] * u[d]) for d in range(3)]
    relaxed = []
    for k in range(27):
        powers = (k // 9, k // 3 % 3, k % 3)
        ones = [d for d in range(3) if powers[d] == 1]
        twos = [d for d in range(3) if powers[d] == 2]
        factor = (1.0 / 3.0) ** len(twos)
        scale = 1.0
        for power in powers:
            scale *= 0.25 if power == 0 else 0.5
        rate = rates[k]
        keep = scale - scale * rate
        if len(ones) == 3:
            relaxed.append(keep * m[k])
            continue
        if len(ones) == 0:
            target = rho
            for d in twos:
                target = target + sq[d]
        elif len(ones) == 1:
            target = j[ones[0]]
        else:
            target = j[ones[0]] * u[ones[1]]
        relaxed.append(keep * m[k] + (scale * factor * rate) * target)
    return along_axes(relaxed, gather_back)


def flow_velocity(g):
    s, d = [], []
    for i in range(9):
        low, mid, high = g[3 * i], g[3 * i + 1], g[3 * i + 2]
        s.append(low + high + 4.0 * mid)
        d.append(high - low)
    ss, ds, sd = [], [], []
    for i in range(3):
        low, mid, high = s[3 * i], s[3 * i + 1], s[3 * i + 2]
        ss.append(low + high + 4.0 * mid)
        ds.append(high - low)
        sd.append(d[3 * i] + d[3 * i + 2] + 4.0 * d[3 * i + 1])
    rho = ss[0] + ss[2] + 4.0 * ss[1]
    inverse = 1.0 / rho
    jx = ss[2] - ss[0]
    jy = ds[0] + ds[2] + 4.0 * ds[1]
    jz = sd[0] + sd[2] + 4.0 * sd[1]
    return jx * inverse, jy * inverse, jz * inverse


def along(velocity, c):
    total = None
    for step, part in zip(c, velocity):
        if step:
            part = part if step > 0 else -part
            total = part if total is None else total + part
    return total


def unit_equilibrium(u):
    base = 1.0 - 1.5 * (u[0] * u[0] + u[1] * u[1] + u[2] * u[2])
    out = [None] * 27
    out[13] = base
    for k in range(14, 27):
        p = along(u, VELOCITIES[k])
        even = base + 4.5 * (p * p)
        odd = 3.0 * p
        out[k] = even + odd
        out[26 - k] = even - odd
    return out


def kernel(n, depth, rows, cells, profiles, pops, kinds, profs, table, rates, out,
           gi, kp, kup, kdn, klow, khigh, vs, vlow, vhigh, forced, bounce, c, yup, ydn, ylow, yhigh, ps, og,
           load_sem, ksend, krecv, send, recv, out_sem):
    me = lax.axis_index("gx")
    last = depth - 1

    def dev(offset):
        return {"gx": lax.rem(me + (n + offset), n)}

    row = lax.broadcasted_iota(jnp.int32, (rows, cells), 0)
    lane = lax.broadcasted_iota(jnp.int32, (rows, cells), 1)

    loads = [pltpu.make_async_copy(pops.at[:, 0, p], gi.at[p], load_sem.at[p]) for p in range(depth)]
    load_kind = pltpu.make_async_copy(kinds.at[0], kp.at[0, pl.ds(1, depth)], load_sem.at[depth])
    load_prof = pltpu.make_async_copy(profs.at[0], kp.at[1, pl.ds(1, depth)], load_sem.at[depth + 1])
    order = [0, last] + list(range(1, last))
    for p in order[:2]:
        loads[p].start()
    load_kind.start()
    load_prof.start()
    for p in order[2:]:
        loads[p].start()

    barrier = pltpu.get_barrier_semaphore()
    offsets = (1, -1, PY, -PY, PY + 1, PY - 1, -PY + 1, -PY - 1)
    for offset in offsets:
        pl.semaphore_signal(barrier, inc=1, device_id=dev(offset), device_id_type=MESH)

    def remote(src, dst, s_sem, r_sem, offset):
        return pltpu.make_async_remote_copy(
            src_ref=src, dst_ref=dst, send_sem=s_sem, recv_sem=r_sem,
            device_id=dev(offset), device_id_type=MESH)

    def low_face(s):
        return [
            remote(c.at[s, 1, pl.ds(0, 9)], c.at[s, depth + 1, pl.ds(0, 9)], send.at[s, 0], recv.at[s, 0], -PY),
            remote(yup.at[s, 1, 0], ylow.at[s, depth + 1, 0], send.at[s, 1], recv.at[s, 1], -PY + 1),
            remote(ydn.at[s, 1, 0], yhigh.at[s, depth + 1, 0], send.at[s, 2], recv.at[s, 2], -PY - 1),
        ]

    def high_face(s):
        return [
            remote(c.at[s, depth, pl.ds(18, 9)], c.at[s, 0, pl.ds(18, 9)], send.at[s, 3], recv.at[s, 3], PY),
            remote(yup.at[s, depth, 2], ylow.at[s, 0, 2], send.at[s, 4], recv.at[s, 4], PY + 1),
            remote(ydn.at[s, depth, 2], yhigh.at[s, 0, 2], send.at[s, 5], recv.at[s, 5], PY - 1),
        ]

    def y_rows(s, first, count, base):
        return [
            remote(yup.at[s, pl.ds(first, count)], ylow.at[s, pl.ds(first, count)], send.at[s, base], recv.at[s, base], 1),
            remote(ydn.at[s, pl.ds(first, count)], yhigh.at[s, pl.ds(first, count)], send.at[s, base + 1], recv.at[s, base + 1], -1),
        ]

    def y_low(s):
        return y_rows(s, 1, 1, 6)

    def y_high(s):
        return y_rows(s, depth, 1, 8)

    def y_mid(s):
        return y_rows(s, 2, depth - 2, 10)

    def kind_messages():
        messages = []
        for i, (src, dst, offset) in enumerate((
            (kp.at[:, 1], kp.at[:, depth + 1], -PY),
            (kp.at[:, depth], kp.at[:, 0], PY),
            (kup.at[pl.ds(1, depth)], klow.at[pl.ds(1, depth)], 1),
            (kdn.at[pl.ds(1, depth)], khigh.at[pl.ds(1, depth)], -1),
            (kup.at[1], klow.at[depth + 1], -PY + 1),
            (kdn.at[1], khigh.at[depth + 1], -PY - 1),
            (kup.at[depth], klow.at[0], PY + 1),
            (kdn.at[depth], khigh.at[0], PY - 1),
        )):
            messages.append(remote(src, dst, ksend.at[i], krecv.at[i], offset))
        return messages

    def collide_plane(s, p, values_of):
        for half in range(cells // 128):
            z = slice(half * 128, half * 128 + 128)
            done = collide(values_of(z), rates)
            for k in range(27):
                c[s, p + 1, k, :, z] = done[k]
                a, b, e = k // 9, k // 3 % 3, k % 3
                if b == 2:
                    yup[s, p + 1, a, e, :, z] = done[k][rows - 1:rows, :]
                elif b == 0:
                    ydn[s, p + 1, a, e, :, z] = done[k][0:1, :]

    def first_collide(p):
        collide_plane(0, p, lambda z: [gi[p, k, :, z] for k in range(27)])

    loads[0].wait()
    first_collide(0)
    pl.semaphore_wait(barrier, len(offsets))
    for message in low_face(0) + y_low(0):
        message.start()
    loads[last].wait()
    first_collide(last)
    for message in high_face(0) + y_high(0):
        message.start()
    load_kind.wait()
    load_prof.wait()
    for p in range(1, depth + 1):
        for i in range(2):
            kup[p, i] = kp[i, p, rows - 1:rows, :]
            kdn[p, i] = kp[i, p, 0:1, :]
    for message in kind_messages():
        message.start()
    for p in range(1, last):
        loads[p].wait()

    @pl.loop(1, last)
    def _(p):
        first_collide(p)

    for message in y_mid(0):
        message.start()

    for message in kind_messages():
        message.wait_recv()

    def looked_up(profile):
        parts = [jnp.zeros(profile.shape, jnp.float32) for _ in range(3)]
        for i in range(profiles):
            hit = profile == i
            parts = [jnp.where(hit, table[i, d], parts[d]) for d in range(3)]
        return parts

    def source_terms(kind, profile):
        velocity = looked_up(profile)
        opened = (kind == 0) | (kind >= 3)
        vent = kind == 2
        terms = [jnp.where(vent, 6.0 * part, 0.0) for part in velocity]
        return terms + [jnp.where(opened, 1.0, 0.0)], velocity

    @pl.loop(0, depth + 2)
    def _(pp):
        terms, velocity = source_terms(kp[0, pp], kp[1, pp])
        inflow = kp[0, pp] == 3
        for d in range(4):
            vs[pp, d] = terms[d]
        for d in range(3):
            forced[pp, d] = jnp.where(inflow, velocity[d], 0.0)
        for rows_in, rows_out in ((klow, vlow), (khigh, vhigh)):
            terms, _ = source_terms(rows_in[pp, 0], rows_in[pp, 1])
            for d in range(4):
                rows_out[pp, d] = terms[d]

    def shifted(value, low_row, high_row, b, e):
        if b == 1:
            value = jnp.where(row == 0, low_row(), pltpu.roll(value, 1, 0))
        elif b == -1:
            value = jnp.where(row == rows - 1, high_row(), pltpu.roll(value, rows - 1, 0))
        if e == 1:
            value = pltpu.roll(value, 1, 1)
        elif e == -1:
            value = pltpu.roll(value, cells - 1, 1)
        return value

    place = lax.rem(me + PY // 2, PY)
    below_outside = (row == 0) & (place == 0)
    above_outside = (row == rows - 1) & (place == PY - 1)

    @pl.loop(0, depth)
    def _(p):
        for k, (a, b, e) in enumerate(VELOCITIES):
            pp = p + 1 - a

            def term(ref):
                total = jnp.zeros((1, cells), jnp.float32)
                moved = along([ref[pp, d] for d in range(3)], (a, b, e))
                total = total if moved is None else moved
                return jnp.where(ref[pp, 3] > 0.5, BIG, total)

            value = shifted(term(vs), lambda: term(vlow), lambda: term(vhigh), b, e)
            if b == 1:
                value = jnp.where(below_outside, 0.0, value)
            elif b == -1:
                value = jnp.where(above_outside, 0.0, value)
            if e == 1:
                value = jnp.where(lane == 0, 0.0, value)
            elif e == -1:
                value = jnp.where(lane == cells - 1, 0.0, value)
            bounce[p, k] = value

    def pull_plane(s, p):
        for k, (a, b, e) in enumerate(VELOCITIES):
            pp = p + 1 - a
            value = shifted(
                c[s, pp, k],
                lambda: ylow[s, pp, a + 1, e + 1],
                lambda: yhigh[s, pp, a + 1, e + 1], b, e)
            extra = bounce[p, k]
            ps[k] = jnp.where(extra > 0.5 * BIG, value, c[s, p + 1, 26 - k] + extra)

    def applied(p, z):
        passed = [ps[k, :, z] for k in range(27)]
        kind = kp[0, p + 1, :, z]
        u = flow_velocity(passed)
        outflow = kind == 4
        u = [jnp.where(outflow, u[d], forced[p + 1, d, :, z]) for d in range(3)]
        feq = unit_equilibrium(u)
        fluid = kind == 0
        return [jnp.where(fluid, passed[k], feq[k]) for k in range(27)]

    def update(s, p):
        pull_plane(s, p)
        collide_plane(s + 1, p, lambda z: applied(p, z))

    def finish(s, p):
        pull_plane(s, p)
        for half in range(cells // 128):
            z = slice(half * 128, half * 128 + 128)
            done = applied(p, z)
            for k in range(27):
                og[p, k, :, z] = done[k]

    def store_out(p):
        return pltpu.make_async_copy(og.at[p], out.at[:, 0, p], out_sem.at[p])

    def arrive(messages):
        for message in messages:
            message.wait_recv()

    def begin(messages):
        for message in messages:
            message.start()

    @pl.loop(0, STEPS - 1)
    def _(s):
        arrive(y_low(s) + y_high(s) + y_mid(s))

        @pl.loop(1, last)
        def _(p):
            update(s, p)

        begin(y_mid(s + 1))
        arrive(low_face(s)[1:] + high_face(s)[1:])
        arrive(high_face(s)[:1])
        update(s, 0)
        begin(low_face(s + 1) + y_low(s + 1))
        arrive(low_face(s)[:1])
        update(s, last)
        begin(high_face(s + 1) + y_high(s + 1))

    s = STEPS - 1
    arrive(y_low(s) + y_high(s) + y_mid(s))

    @pl.loop(1, last)
    def _(p):
        finish(s, p)
        store_out(p).start()

    arrive(low_face(s)[1:] + high_face(s)[1:])
    arrive(high_face(s)[:1])
    finish(s, 0)
    store_out(0).start()
    arrive(low_face(s)[:1])
    finish(s, last)
    store_out(last).start()

    for message in kind_messages():
        message.wait_send()
    for s in range(STEPS):
        for message in low_face(s) + high_face(s) + y_low(s) + y_high(s) + y_mid(s):
            message.wait_send()
    for p in range(depth):
        store_out(p).wait()


def solution(mesh):
    n = mesh.shape["gx"]

    def local(populations, cell_kind, profile, vent_table, rates):
        depth, rows, cells = populations.shape[2:]
        profiles = vent_table.shape[0]
        f32, i32 = jnp.float32, jnp.int32
        outer = depth + 2
        vm = pltpu.VMEM
        dma = pltpu.SemaphoreType.DMA

        def body(*refs):
            kernel(n, depth, rows, cells, profiles, *refs)

        return pl.pallas_call(
            body,
            out_shape=jax.ShapeDtypeStruct(populations.shape, f32),
            in_specs=[
                pl.BlockSpec(memory_space=pl.ANY),
                pl.BlockSpec(memory_space=pl.ANY),
                pl.BlockSpec(memory_space=pl.ANY),
                pl.BlockSpec(memory_space=pltpu.SMEM),
                pl.BlockSpec(memory_space=pltpu.SMEM),
            ],
            out_specs=pl.BlockSpec(memory_space=pl.ANY),
            scratch_shapes=[
                vm((depth, 27, rows, cells), f32),
                vm((2, outer, rows, cells), i32),
                vm((outer, 2, 1, cells), i32),
                vm((outer, 2, 1, cells), i32),
                vm((outer, 2, 1, cells), i32),
                vm((outer, 2, 1, cells), i32),
                vm((outer, 4, rows, cells), f32),
                vm((outer, 4, 1, cells), f32),
                vm((outer, 4, 1, cells), f32),
                vm((outer, 3, rows, cells), f32),
                vm((depth, 27, rows, cells), f32),
                vm((STEPS, outer, 27, rows, cells), f32),
                vm((STEPS, outer, 3, 3, 1, cells), f32),
                vm((STEPS, outer, 3, 3, 1, cells), f32),
                vm((STEPS, outer, 3, 3, 1, cells), f32),
                vm((STEPS, outer, 3, 3, 1, cells), f32),
                vm((27, rows, cells), f32),
                vm((depth, 27, rows, cells), f32),
                dma((depth + 2,)),
                dma((8,)),
                dma((8,)),
                dma((STEPS, 12)),
                dma((STEPS, 12)),
                dma((depth,)),
            ],
            compiler_params=pltpu.CompilerParams(collective_id=0, has_side_effects=True),
        )(populations, cell_kind, profile, vent_table, rates)

    return jax.shard_map(
        local,
        mesh=mesh,
        in_specs=(
            P("scen", "gx", None, None, None),
            P("gx", None, None, "scen"),
            P("gx", None, None, "scen"),
            P("scen", None),
            P(),
        ),
        out_specs=P("scen", "gx", None, None, None),
        check_vma=False,
    )
```

profile of v0, /device:TPU:0, one launch (start us, length us, event | category | flops | bytes accessed | tf_op | source)
XLA Modules:
  0.0 39.7 jit_solution(2381051959732032209)
XLA Ops:
  0.0 1.3 %copy.6.refs_3_ = f32[8,3]{1,0:T(8,128)} copy(f32[8,3]{0,1:T(4,128)} %param.8) | data formatting | bytes 192 | tf_op args[3]
  1.3 36.2 %shard_map.55 = f32[27,1,4,8,256]{4,3,2,1,0:T(8,128)} custom-call(f32[27,1,4,8,256]{4,3,2,1,0:T(8,128)} %refs_0_.1, s32[1,4,8,256]{3,2,1,0:T(8,128)} %refs_1_.1, s32[1,4,8,256]{3,2,1,0:T(8,128)} %refs_2_.1, f32[8,3]{1,0:T(8,128)} %copy.6.refs_3_, f32[27]{0:T(128)} %refs_4_.1), custom_call_target="tpu_custom_call" | custom-call | tf_op jit(solution)/shard_map/pallas_call | solution.py:396
  37.5 2.2 %copy.8 = f32[27,1,4,8,256]{4,3,2,1,0:T(8,128)} copy(f32[27,1,4,8,256]{4,3,2,1,0:T(8,128)} %shard_map.55) | data formatting | bytes 1769472
where the time goes:
time: 40.2 us; the launch traced here: 39.7 us
  Pallas kernels  36.2 us (90%)
  local copies, waits for them, and re-layouts  3.52 us (9%)
    pallas_call x1, Pallas kernels, local(): pl.pallas_call(body, out_shape=jax.ShapeDtypeStruct(populations.shape, f3...  36.2 us
    unnamed x2, local copies, waits for them, and re-layouts  3.52 us

commit v1 on v0

--- a/solution.py
+++ b/solution.py
@@ -108,14 +108,19 @@
     return out
 
 
-def kernel(n, depth, rows, cells, profiles, pops, kinds, profs, table, rates, out,
-           gi, kp, kup, kdn, klow, khigh, vs, vlow, vhigh, forced, bounce, c, yup, ydn, ylow, yhigh, ps, og,
+def kernel(n, depth, rows, cells, profiles, pops, kinds, profs, table_in, rates_in, out,
+           table, rates, gi, kp, kup, kdn, klow, khigh, vs, vlow, vhigh, forced, bounce, c, yup, ydn, ylow, yhigh, ps, og,
            load_sem, ksend, krecv, send, recv, out_sem):
     me = lax.axis_index("gx")
     last = depth - 1
 
     def dev(offset):
         return {"gx": lax.rem(me + (n + offset), n)}
+
+    barrier = pltpu.get_barrier_semaphore()
+    offsets = (1, -1, PY, -PY, PY + 1, PY - 1, -PY + 1, -PY - 1)
+    for offset in offsets:
+        pl.semaphore_signal(barrier, inc=1, device_id=dev(offset), device_id_type=MESH)
 
     row = lax.broadcasted_iota(jnp.int32, (rows, cells), 0)
     lane = lax.broadcasted_iota(jnp.int32, (rows, cells), 1)
@@ -124,17 +129,14 @@
     load_kind = pltpu.make_async_copy(kinds.at[0], kp.at[0, pl.ds(1, depth)], load_sem.at[depth])
     load_prof = pltpu.make_async_copy(profs.at[0], kp.at[1, pl.ds(1, depth)], load_sem.at[depth + 1])
     order = [0, last] + list(range(1, last))
-    for p in order[:2]:
-        loads[p].start()
+    load_rates = pltpu.make_async_copy(rates_in, rates, load_sem.at[depth + 2])
+    load_table = pltpu.make_async_copy(table_in, table, load_sem.at[depth + 3])
     load_kind.start()
     load_prof.start()
-    for p in order[2:]:
+    load_rates.start()
+    load_table.start()
+    for p in order:
         loads[p].start()
-
-    barrier = pltpu.get_barrier_semaphore()
-    offsets = (1, -1, PY, -PY, PY + 1, PY - 1, -PY + 1, -PY - 1)
-    for offset in offsets:
-        pl.semaphore_signal(barrier, inc=1, device_id=dev(offset), device_id_type=MESH)
 
     def remote(src, dst, s_sem, r_sem, offset):
         return pltpu.make_async_remote_copy(
@@ -143,16 +145,20 @@
 
     def low_face(s):
         return [
-            remote(c.at[s, 1, pl.ds(0, 9)], c.at[s, depth + 1, pl.ds(0, 9)], send.at[s, 0], recv.at[s, 0], -PY),
             remote(yup.at[s, 1, 0], ylow.at[s, depth + 1, 0], send.at[s, 1], recv.at[s, 1], -PY + 1),
             remote(ydn.at[s, 1, 0], yhigh.at[s, depth + 1, 0], send.at[s, 2], recv.at[s, 2], -PY - 1),
+            remote(c.at[s, 1, pl.ds(0, 3), pl.ds(1, rows - 1)], c.at[s, depth + 1, pl.ds(0, 3), pl.ds(1, rows - 1)], send.at[s, 0], recv.at[s, 0], -PY),
+            remote(c.at[s, 1, pl.ds(3, 3)], c.at[s, depth + 1, pl.ds(3, 3)], send.at[s, 12], recv.at[s, 12], -PY),
+            remote(c.at[s, 1, pl.ds(6, 3), pl.ds(0, rows - 1)], c.at[s, depth + 1, pl.ds(6, 3), pl.ds(0, rows - 1)], send.at[s, 13], recv.at[s, 13], -PY),
         ]
 
     def high_face(s):
         return [
-            remote(c.at[s, depth, pl.ds(18, 9)], c.at[s, 0, pl.ds(18, 9)], send.at[s, 3], recv.at[s, 3], PY),
             remote(yup.at[s, depth, 2], ylow.at[s, 0, 2], send.at[s, 4], recv.at[s, 4], PY + 1),
             remote(ydn.at[s, depth, 2], yhigh.at[s, 0, 2], send.at[s, 5], recv.at[s, 5], PY - 1),
+            remote(c.at[s, depth, pl.ds(18, 3), pl.ds(1, rows - 1)], c.at[s, 0, pl.ds(18, 3), pl.ds(1, rows - 1)], send.at[s, 3], recv.at[s, 3], PY),
+            remote(c.at[s, depth, pl.ds(21, 3)], c.at[s, 0, pl.ds(21, 3)], send.at[s, 14], recv.at[s, 14], PY),
+            remote(c.at[s, depth, pl.ds(24, 3), pl.ds(0, rows - 1)], c.at[s, 0, pl.ds(24, 3), pl.ds(0, rows - 1)], send.at[s, 15], recv.at[s, 15], PY),
         ]
 
     def y_rows(s, first, count, base):
@@ -185,6 +191,14 @@
             messages.append(remote(src, dst, ksend.at[i], krecv.at[i], offset))
         return messages
 
+    def arrive(messages):
+        for message in messages:
+            message.wait_recv()
+
+    def begin(messages):
+        for message in messages:
+            message.start()
+
     def collide_plane(s, p, values_of):
         for half in range(cells // 128):
             z = slice(half * 128, half * 128 + 128)
@@ -200,23 +214,22 @@
     def first_collide(p):
         collide_plane(0, p, lambda z: [gi[p, k, :, z] for k in range(27)])
 
-    loads[0].wait()
-    first_collide(0)
-    pl.semaphore_wait(barrier, len(offsets))
-    for message in low_face(0) + y_low(0):
-        message.start()
-    loads[last].wait()
-    first_collide(last)
-    for message in high_face(0) + y_high(0):
-        message.start()
     load_kind.wait()
     load_prof.wait()
     for p in range(1, depth + 1):
         for i in range(2):
             kup[p, i] = kp[i, p, rows - 1:rows, :]
             kdn[p, i] = kp[i, p, 0:1, :]
-    for message in kind_messages():
-        message.start()
+    load_rates.wait()
+    load_table.wait()
+    loads[0].wait()
+    first_collide(0)
+    pl.semaphore_wait(barrier, len(offsets))
+    begin(kind_messages())
+    begin(y_low(0) + low_face(0))
+    loads[last].wait()
+    first_collide(last)
+    begin(y_high(0) + high_face(0))
     for p in range(1, last):
         loads[p].wait()
 
@@ -234,7 +247,7 @@
         parts = [jnp.zeros(profile.shape, jnp.float32) for _ in range(3)]
         for i in range(profiles):
             hit = profile == i
-            parts = [jnp.where(hit, table[i, d], parts[d]) for d in range(3)]
+            parts = [jnp.where(hit, table[d, i], parts[d]) for d in range(3)]
         return parts
 
     def source_terms(kind, profile):
@@ -329,46 +342,33 @@
     def store_out(p):
         return pltpu.make_async_copy(og.at[p], out.at[:, 0, p], out_sem.at[p])
 
-    def arrive(messages):
-        for message in messages:
-            message.wait_recv()
-
-    def begin(messages):
-        for message in messages:
-            message.start()
-
-    @pl.loop(0, STEPS - 1)
-    def _(s):
+    low = (low_face, y_low, 0, last)
+    high = (high_face, y_high, last, 0)
+    faces = [low, high]
+    for s in range(STEPS):
         arrive(y_low(s) + y_high(s) + y_mid(s))
 
         @pl.loop(1, last)
         def _(p):
-            update(s, p)
-
-        begin(y_mid(s + 1))
-        arrive(low_face(s)[1:] + high_face(s)[1:])
-        arrive(high_face(s)[:1])
-        update(s, 0)
-        begin(low_face(s + 1) + y_low(s + 1))
-        arrive(low_face(s)[:1])
-        update(s, last)
-        begin(high_face(s + 1) + y_high(s + 1))
-
-    s = STEPS - 1
-    arrive(y_low(s) + y_high(s) + y_mid(s))
-
-    @pl.loop(1, last)
-    def _(p):
-        finish(s, p)
-        store_out(p).start()
-
-    arrive(low_face(s)[1:] + high_face(s)[1:])
-    arrive(high_face(s)[:1])
-    finish(s, 0)
-    store_out(0).start()
-    arrive(low_face(s)[:1])
-    finish(s, last)
-    store_out(last).start()
+            if s < STEPS - 1:
+                update(s, p)
+            else:
+                finish(s, p)
+                store_out(p).start()
+
+        if s < STEPS - 1:
+            begin(y_mid(s + 1))
+        for face in faces:
+            arrive(face[0](s))
+            p = face[3]
+            if s < STEPS - 1:
+                update(s, p)
+                leaves = low if p == 0 else high
+                begin(leaves[1](s + 1) + leaves[0](s + 1))
+            else:
+                finish(s, p)
+                store_out(p).start()
+        faces = faces[::-1]
 
     for message in kind_messages():
         message.wait_send()
@@ -400,11 +400,13 @@
                 pl.BlockSpec(memory_space=pl.ANY),
                 pl.BlockSpec(memory_space=pl.ANY),
                 pl.BlockSpec(memory_space=pl.ANY),
-                pl.BlockSpec(memory_space=pltpu.SMEM),
-                pl.BlockSpec(memory_space=pltpu.SMEM),
+                pl.BlockSpec(memory_space=pl.ANY),
+                pl.BlockSpec(memory_space=pl.ANY),
             ],
             out_specs=pl.BlockSpec(memory_space=pl.ANY),
             scratch_shapes=[
+                pltpu.SMEM((3, profiles), f32),
+                pltpu.SMEM((27,), f32),
                 vm((depth, 27, rows, cells), f32),
                 vm((2, outer, rows, cells), i32),
                 vm((outer, 2, 1, cells), i32),
@@ -423,15 +425,15 @@
                 vm((STEPS, outer, 3, 3, 1, cells), f32),
                 vm((27, rows, cells), f32),
                 vm((depth, 27, rows, cells), f32),
-                dma((depth + 2,)),
+                dma((depth + 4,)),
                 dma((8,)),
                 dma((8,)),
-                dma((STEPS, 12)),
-                dma((STEPS, 12)),
+                dma((STEPS, 16)),
+                dma((STEPS, 16)),
                 dma((depth,)),
             ],
             compiler_params=pltpu.CompilerParams(collective_id=0, has_side_effects=True),
-        )(populations, cell_kind, profile, vent_table, rates)
+        )(populations, cell_kind, profile, vent_table.T, rates)
 
     return jax.shard_map(
         local,

time: 40.2 us -> 34.4 us (0.86)
  Pallas kernels: 36.2 us -> 32 us
  local copies, waits for them, and re-layouts: 3.52 us -> 2.17 us
    pallas_call x1, Pallas kernels: 36.2 us -> 32 us  [local(): pl.pallas_call(body, out_shape=jax.ShapeDtypeStruct(populations.shape, f3...]
    unnamed x2 -> x1, local copies, waits for them, and re-layouts: 3.52 us -> 2.17 us
where the time goes in v1:
time: 34.4 us; the launch traced here: 34.2 us
  Pallas kernels  32 us (93%)
  local copies, waits for them, and re-layouts  2.17 us (6%)
    pallas_call x1, Pallas kernels, local(): pl.pallas_call(body, out_shape=jax.ShapeDtypeStruct(populations.shape, f3...  32 us
    unnamed x1, local copies, waits for them, and re-layouts  2.17 us

profile of v1, /device:TPU:0, one launch (start us, length us, event | category | flops | bytes accessed | tf_op | source)
XLA Modules:
  0.0 34.2 jit_solution(3994599862895271307)
XLA Ops:
  0.0 32.0 %shard_map.55 = f32[27,1,4,8,256]{4,3,2,1,0:T(8,128)} custom-call(f32[27,1,4,8,256]{4,3,2,1,0:T(8,128)} %refs_0_.1, s32[1,4,8,256]{3,2,1,0:T(8,128)} %refs_1_.1, s32[1,4,8,256]{3,2,1,0:T(8,128)} %refs_2_.1, f32[3,8]{1,0:T(4,128)} %bitcast.1, f32[27]{0:T(128)} %refs_4_.1), custom_call_target="tpu_custom_call" | custom-call | tf_op jit(solution)/shard_map/pallas_call | solution.py:396
  32.0 2.2 %copy.7 = f32[27,1,4,8,256]{4,3,2,1,0:T(8,128)} copy(f32[27,1,4,8,256]{4,3,2,1,0:T(8,128)} %shard_map.55) | data formatting | bytes 1769472

commit v2 on v1

--- a/solution.py
+++ b/solution.py
@@ -109,8 +109,8 @@
 
 
 def kernel(n, depth, rows, cells, profiles, pops, kinds, profs, table_in, rates_in, out,
-           table, rates, gi, kp, kup, kdn, klow, khigh, vs, vlow, vhigh, forced, bounce, c, yup, ydn, ylow, yhigh, ps, og,
-           load_sem, ksend, krecv, send, recv, out_sem):
+           table, rates, gi, kp, kup, kdn, klow, khigh, vs, vlow, vhigh, forced, bounce, c, yup, ydn, ylow, yhigh, ps,
+           load_sem, ksend, krecv, send, recv):
     me = lax.axis_index("gx")
     last = depth - 1
 
@@ -161,32 +161,32 @@
             remote(c.at[s, depth, pl.ds(24, 3), pl.ds(0, rows - 1)], c.at[s, 0, pl.ds(24, 3), pl.ds(0, rows - 1)], send.at[s, 15], recv.at[s, 15], PY),
         ]
 
-    def y_rows(s, first, count, base):
+    def y_rows(s, planes, dirs, base):
         return [
-            remote(yup.at[s, pl.ds(first, count)], ylow.at[s, pl.ds(first, count)], send.at[s, base], recv.at[s, base], 1),
-            remote(ydn.at[s, pl.ds(first, count)], yhigh.at[s, pl.ds(first, count)], send.at[s, base + 1], recv.at[s, base + 1], -1),
+            remote(yup.at[s, planes, dirs], ylow.at[s, planes, dirs], send.at[s, base], recv.at[s, base], 1),
+            remote(ydn.at[s, planes, dirs], yhigh.at[s, planes, dirs], send.at[s, base + 1], recv.at[s, base + 1], -1),
         ]
 
     def y_low(s):
-        return y_rows(s, 1, 1, 6)
+        return y_rows(s, 1, pl.ds(1, 2), 6)
 
     def y_high(s):
-        return y_rows(s, depth, 1, 8)
+        return y_rows(s, depth, pl.ds(0, 2), 8)
 
     def y_mid(s):
-        return y_rows(s, 2, depth - 2, 10)
+        return y_rows(s, pl.ds(2, depth - 2), pl.ds(0, 3), 10)
 
     def kind_messages():
         messages = []
         for i, (src, dst, offset) in enumerate((
-            (kp.at[:, 1], kp.at[:, depth + 1], -PY),
-            (kp.at[:, depth], kp.at[:, 0], PY),
+            (kp.at[0, 1], kp.at[0, depth + 1], -PY),
+            (kp.at[0, depth], kp.at[0, 0], PY),
             (kup.at[pl.ds(1, depth)], klow.at[pl.ds(1, depth)], 1),
             (kdn.at[pl.ds(1, depth)], khigh.at[pl.ds(1, depth)], -1),
-            (kup.at[1], klow.at[depth + 1], -PY + 1),
-            (kdn.at[1], khigh.at[depth + 1], -PY - 1),
-            (kup.at[depth], klow.at[0], PY + 1),
-            (kdn.at[depth], khigh.at[0], PY - 1),
+            (kup.at[1, 0], klow.at[depth + 1, 0], -PY + 1),
+            (kdn.at[1, 0], khigh.at[depth + 1, 0], -PY - 1),
+            (kup.at[depth, 0], klow.at[0, 0], PY + 1),
+            (kdn.at[depth, 0], khigh.at[0, 0], PY - 1),
         )):
             messages.append(remote(src, dst, ksend.at[i], krecv.at[i], offset))
         return messages
@@ -199,10 +199,12 @@
         for message in messages:
             message.start()
 
-    def collide_plane(s, p, values_of):
+    def collide_plane(s, p, values_of, adjust=None):
         for half in range(cells // 128):
             z = slice(half * 128, half * 128 + 128)
             done = collide(values_of(z), rates)
+            if adjust is not None:
+                done = adjust(done, z)
             for k in range(27):
                 c[s, p + 1, k, :, z] = done[k]
                 a, b, e = k // 9, k // 3 % 3, k % 3
@@ -211,8 +213,18 @@
                 elif b == 0:
                     ydn[s, p + 1, a, e, :, z] = done[k][0:1, :]
 
-    def first_collide(p):
-        collide_plane(0, p, lambda z: [gi[p, k, :, z] for k in range(27)])
+    def first_collide(p, side=None):
+        def adjust(done, z):
+            solid = vs[p + 1, 3, :, z] < 0.5
+            velocity = [vs[p + 1, d, :, z] for d in range(3)]
+            done = list(done)
+            for k, c_k in enumerate(VELOCITIES):
+                if c_k[0] == side:
+                    done[k] = jnp.where(solid, along(velocity, c_k), done[k])
+            return done
+
+        collide_plane(0, p, lambda z: [gi[p, k, :, z] for k in range(27)],
+                      None if side is None else adjust)
 
     load_kind.wait()
     load_prof.wait()
@@ -220,29 +232,6 @@
         for i in range(2):
             kup[p, i] = kp[i, p, rows - 1:rows, :]
             kdn[p, i] = kp[i, p, 0:1, :]
-    load_rates.wait()
-    load_table.wait()
-    loads[0].wait()
-    first_collide(0)
-    pl.semaphore_wait(barrier, len(offsets))
-    begin(kind_messages())
-    begin(y_low(0) + low_face(0))
-    loads[last].wait()
-    first_collide(last)
-    begin(y_high(0) + high_face(0))
-    for p in range(1, last):
-        loads[p].wait()
-
-    @pl.loop(1, last)
-    def _(p):
-        first_collide(p)
-
-    for message in y_mid(0):
-        message.start()
-
-    for message in kind_messages():
-        message.wait_recv()
-
     def looked_up(profile):
         parts = [jnp.zeros(profile.shape, jnp.float32) for _ in range(3)]
         for i in range(profiles):
@@ -257,7 +246,10 @@
         terms = [jnp.where(vent, 6.0 * part, 0.0) for part in velocity]
         return terms + [jnp.where(opened, 1.0, 0.0)], velocity
 
-    @pl.loop(0, depth + 2)
+    load_rates.wait()
+    load_table.wait()
+
+    @pl.loop(1, depth + 1)
     def _(pp):
         terms, velocity = source_terms(kp[0, pp], kp[1, pp])
         inflow = kp[0, pp] == 3
@@ -265,6 +257,37 @@
             vs[pp, d] = terms[d]
         for d in range(3):
             forced[pp, d] = jnp.where(inflow, velocity[d], 0.0)
+
+    loads[0].wait()
+    first_collide(0, -1)
+    pl.semaphore_wait(barrier, len(offsets))
+    begin(kind_messages())
+    begin(y_low(0) + low_face(0))
+    loads[last].wait()
+    first_collide(last, 1)
+    begin(y_high(0) + high_face(0))
+    for p in range(1, last):
+        loads[p].wait()
+
+    @pl.loop(1, last)
+    def _(p):
+        first_collide(p)
+
+    for message in y_mid(0):
+        message.start()
+
+    for message in kind_messages():
+        message.wait_recv()
+
+    for pp in (0, depth + 1):
+        kind = kp[0, pp]
+        vs[pp, 3] = jnp.where((kind == 0) | (kind >= 3), 1.0, 0.0)
+        for rows_in, rows_out in ((klow, vlow), (khigh, vhigh)):
+            kind = rows_in[pp, 0]
+            rows_out[pp, 3] = jnp.where((kind == 0) | (kind >= 3), 1.0, 0.0)
+
+    @pl.loop(1, depth + 1)
+    def _(pp):
         for rows_in, rows_out in ((klow, vlow), (khigh, vhigh)):
             terms, _ = source_terms(rows_in[pp, 0], rows_in[pp, 1])
             for d in range(4):
@@ -285,18 +308,25 @@
     below_outside = (row == 0) & (place == 0)
     above_outside = (row == rows - 1) & (place == PY - 1)
 
-    @pl.loop(0, depth)
-    def _(p):
+    def bounce_plane(p, steps_x):
         for k, (a, b, e) in enumerate(VELOCITIES):
+            if a not in steps_x:
+                continue
             pp = p + 1 - a
-
-            def term(ref):
-                total = jnp.zeros((1, cells), jnp.float32)
-                moved = along([ref[pp, d] for d in range(3)], (a, b, e))
-                total = total if moved is None else moved
+            outer = isinstance(pp, int) and pp in (0, depth + 1)
+
+            def term(ref, sent):
+                if outer:
+                    total = sent
+                else:
+                    total = along([ref[pp, d] for d in range(3)], (a, b, e))
+                    total = jnp.zeros((1, cells), jnp.float32) if total is None else total
                 return jnp.where(ref[pp, 3] > 0.5, BIG, total)
 
-            value = shifted(term(vs), lambda: term(vlow), lambda: term(vhigh), b, e)
+            value = shifted(
+                term(vs, c[0, pp, k] if outer else None),
+                lambda: term(vlow, ylow[0, pp, a + 1, e + 1] if outer else None),
+                lambda: term(vhigh, yhigh[0, pp, a + 1, e + 1] if outer else None), b, e)
             if b == 1:
                 value = jnp.where(below_outside, 0.0, value)
             elif b == -1:
@@ -307,6 +337,13 @@
                 value = jnp.where(lane == cells - 1, 0.0, value)
             bounce[p, k] = value
 
+    @pl.loop(1, last)
+    def _(p):
+        bounce_plane(p, (-1, 0, 1))
+
+    bounce_plane(0, (-1, 0))
+    bounce_plane(last, (0, 1))
+
     def pull_plane(s, p):
         for k, (a, b, e) in enumerate(VELOCITIES):
             pp = p + 1 - a
@@ -337,10 +374,7 @@
             z = slice(half * 128, half * 128 + 128)
             done = applied(p, z)
             for k in range(27):
-                og[p, k, :, z] = done[k]
-
-    def store_out(p):
-        return pltpu.make_async_copy(og.at[p], out.at[:, 0, p], out_sem.at[p])
+                out[k, 0, p, :, z] = done[k]
 
     low = (low_face, y_low, 0, last)
     high = (high_face, y_high, last, 0)
@@ -354,20 +388,20 @@
                 update(s, p)
             else:
                 finish(s, p)
-                store_out(p).start()
 
         if s < STEPS - 1:
             begin(y_mid(s + 1))
         for face in faces:
             arrive(face[0](s))
             p = face[3]
+            if s == 0:
+                bounce_plane(p, (1,) if p == 0 else (-1,))
             if s < STEPS - 1:
                 update(s, p)
                 leaves = low if p == 0 else high
                 begin(leaves[1](s + 1) + leaves[0](s + 1))
             else:
                 finish(s, p)
-                store_out(p).start()
         faces = faces[::-1]
 
     for message in kind_messages():
@@ -375,8 +409,6 @@
     for s in range(STEPS):
         for message in low_face(s) + high_face(s) + y_low(s) + y_high(s) + y_mid(s):
             message.wait_send()
-    for p in range(depth):
-        store_out(p).wait()
 
 
 def solution(mesh):
@@ -395,7 +427,7 @@
 
         return pl.pallas_call(
             body,
-            out_shape=jax.ShapeDtypeStruct(populations.shape, f32),
+            out_shape=pltpu.VMEM(populations.shape, f32),
             in_specs=[
                 pl.BlockSpec(memory_space=pl.ANY),
                 pl.BlockSpec(memory_space=pl.ANY),
@@ -403,7 +435,7 @@
                 pl.BlockSpec(memory_space=pl.ANY),
                 pl.BlockSpec(memory_space=pl.ANY),
             ],
-            out_specs=pl.BlockSpec(memory_space=pl.ANY),
+            out_specs=pl.BlockSpec(memory_space=pltpu.VMEM),
             scratch_shapes=[
                 pltpu.SMEM((3, profiles), f32),
                 pltpu.SMEM((27,), f32),
@@ -424,16 +456,14 @@
                 vm((STEPS, outer, 3, 3, 1, cells), f32),
                 vm((STEPS, outer, 3, 3, 1, cells), f32),
                 vm((27, rows, cells), f32),
-                vm((depth, 27, rows, cells), f32),
                 dma((depth + 4,)),
                 dma((8,)),
                 dma((8,)),
                 dma((STEPS, 16)),
                 dma((STEPS, 16)),
-                dma((depth,)),
             ],
-            compiler_params=pltpu.CompilerParams(collective_id=0, has_side_effects=True),
-        )(populations, cell_kind, profile, vent_table.T, rates)
+            compiler_params=pltpu.CompilerParams(collective_id=0, has_side_effects=True, vmem_limit_bytes=32*1024*1024),
+        )(*[pltpu.with_memory_space_constraint(x, pltpu.HBM) for x in (populations, cell_kind, profile, vent_table.T, rates)])
 
     return jax.shard_map(
         local,

time: 34.4 us -> 31.4 us (0.913)
  Pallas kernels: 32 us -> 30.3 us
  local copies, waits for them, and re-layouts: 2.17 us -> 0.91 us
    pallas_call x1, Pallas kernels: 32 us -> 30.3 us  [local(): pl.pallas_call(body, out_shape=pltpu.VMEM(populations.shape, f32), in_spe...]
    unnamed x1, local copies, waits for them, and re-layouts: 2.17 us -> 0.91 us
where the time goes in v2:
time: 31.4 us; the launch traced here: 31.2 us
  Pallas kernels  30.3 us (96%)
  local copies, waits for them, and re-layouts  0.91 us (3%)
    pallas_call x1, Pallas kernels, local(): pl.pallas_call(body, out_shape=pltpu.VMEM(populations.shape, f32), in_spe...  30.3 us
    unnamed x1, local copies, waits for them, and re-layouts  0.91 us

profile of v2, /device:TPU:0, one launch (start us, length us, event | category | flops | bytes accessed | tf_op | source)
XLA Modules:
  0.0 31.2 jit_solution(14810993821440876949)
XLA Ops:
  0.0 30.3 %shard_map.55 = f32[27,1,4,8,256]{4,3,2,1,0:T(8,128)S(1)} custom-call(f32[27,1,4,8,256]{4,3,2,1,0:T(8,128)} %refs_0_.1, s32[1,4,8,256]{3,2,1,0:T(8,128)} %refs_1_.1, s32[1,4,8,256]{3,2,1,0:T(8,128)} %refs_2_.1, f32[3,8]{1,0:T(4,128)} %bitcast.1, f32[27]{0:T(128)} %refs_4_.1), custom_call_target="tpu_custom_call" | custom-call | tf_op jit(solution)/shard_map/pallas_call | solution.py:428
  30.3 0.9 %copy.7 = f32[27,1,4,8,256]{4,3,2,1,0:T(8,128)} copy(f32[27,1,4,8,256]{4,3,2,1,0:T(8,128)S(1)} %shard_map.55) | data formatting | bytes 1769472

commit v3 on v2

--- a/solution.py
+++ b/solution.py
@@ -260,12 +260,8 @@
 
     loads[0].wait()
     first_collide(0, -1)
-    pl.semaphore_wait(barrier, len(offsets))
-    begin(kind_messages())
-    begin(y_low(0) + low_face(0))
     loads[last].wait()
     first_collide(last, 1)
-    begin(y_high(0) + high_face(0))
     for p in range(1, last):
         loads[p].wait()
 
@@ -273,8 +269,11 @@
     def _(p):
         first_collide(p)
 
-    for message in y_mid(0):
-        message.start()
+    pl.semaphore_wait(barrier, len(offsets))
+    begin(kind_messages())
+    begin(y_mid(0) + y_low(0) + y_high(0))
+    begin(low_face(0))
+    begin(high_face(0))
 
     for message in kind_messages():
         message.wait_recv()

time: 31.4 us -> 30.3 us (0.965)
  Pallas kernels: 30.3 us -> 29.2 us
    pallas_call x1, Pallas kernels: 30.3 us -> 29.2 us  [local(): pl.pallas_call(body, out_shape=pltpu.VMEM(populations.shape, f32), in_spe...]
where the time goes in v3:
time: 30.3 us; the launch traced here: 30.2 us
  Pallas kernels  29.2 us (96%)
  local copies, waits for them, and re-layouts  0.91 us (3%)
    pallas_call x1, Pallas kernels, local(): pl.pallas_call(body, out_shape=pltpu.VMEM(populations.shape, f32), in_spe...  29.2 us
    unnamed x1, local copies, waits for them, and re-layouts  0.91 us

profile of v3, /device:TPU:0, one launch (start us, length us, event | category | flops | bytes accessed | tf_op | source)
XLA Modules:
  0.0 30.2 jit_solution(12192163759063530057)
XLA Ops:
  0.0 29.2 %shard_map.55 = f32[27,1,4,8,256]{4,3,2,1,0:T(8,128)S(1)} custom-call(f32[27,1,4,8,256]{4,3,2,1,0:T(8,128)} %refs_0_.1, s32[1,4,8,256]{3,2,1,0:T(8,128)} %refs_1_.1, s32[1,4,8,256]{3,2,1,0:T(8,128)} %refs_2_.1, f32[3,8]{1,0:T(4,128)} %bitcast.1, f32[27]{0:T(128)} %refs_4_.1), custom_call_target="tpu_custom_call" | custom-call | tf_op jit(solution)/shard_map/pallas_call | solution.py:427
  29.2 0.9 %copy.7 = f32[27,1,4,8,256]{4,3,2,1,0:T(8,128)} copy(f32[27,1,4,8,256]{4,3,2,1,0:T(8,128)S(1)} %shard_map.55) | data formatting | bytes 1769472
